TPU v7x, 32 devices: a whole 2x2x4 slice. The times are simulated.
32 devices in a mesh: row: 4 (over y, x), col: 8 (over z, core).
Axes of the slice: x: 2, y: 2, z: 4, core: 2. Of those that a mesh axis runs over, the one named last changes fastest.
Arguments:
- operator: float32 [4096, 4096], P('row', 'col'), may hold values from -0.09375 to 0.09375
- state: float32 [4096, 4096], P('row', 'col'), may hold values from -60 to 60, as said below
- source: float32 [4096, 4096], P('row', 'col'), may hold values from -60 to 60, as said below
Outputs:
- state_next: float32 [4096, 4096], P('row', 'col')
- operator_fourth: float32 [4096, 4096], P('row', 'col')
Inputs may be any that keep to these rules, and one draw needn't show every extreme that they name: symmetric: state equals its transpose. symmetric: source equals its transpose.
All inputs are finite; a program needn't handle non-finite values.
Results may differ from a plain program's by a relative error of at most 0.000098.
Values sent between devices are 32-bit elements; how exact they have to be, the bound alone decides.
No kernel may reach another device: no remote copies, remote signals or barrier semaphores. Data moves between devices by JAX's collectives and lax.ppermute only.
A program may use at most 128 MiB of HBM per device.

v0:
```python
import jax
import jax.numpy as jnp
from jax import lax
from jax.sharding import PartitionSpec as P


def matmul(left, right):
    return jnp.dot(left, right, preferred_element_type=jnp.float32, precision=lax.Precision.HIGHEST)


def split_pieces(block, groups):
    rows, columns = block.shape
    width = columns // groups
    pieces = block.reshape(2, columns, groups, width).transpose(2, 0, 3, 1)
    return pieces.reshape(2 * groups, width, columns)


def join_pieces(pieces, groups):
    count, width, columns = pieces.shape
    joined = pieces.reshape(groups, 2, width, columns).transpose(1, 0, 2, 3)
    return joined.reshape(2 * groups * width, columns)


def folder(panel, piece):
    return matmul(panel, piece)


def on_device(operator, state, source):
    groups = lax.axis_size("row")
    row_panel = lax.all_gather(operator, "col", axis=1, tiled=True)
    product = matmul(row_panel, lax.all_gather(state, "row", axis=0, tiled=True))
    square = matmul(row_panel, lax.all_gather(operator, "row", axis=0, tiled=True))
    moved = lax.all_to_all(
        lax.all_to_all(
            split_pieces(product, groups), "row", split_axis=0, concat_axis=0, tiled=True
        ),
        "col",
        split_axis=0,
        concat_axis=0,
        tiled=True,
    )
    turned = join_pieces(
        lax.all_to_all(moved, "row", split_axis=0, concat_axis=0, tiled=True), groups
    )
    state_next = folder(row_panel, lax.all_gather(turned, "row", axis=0, tiled=True)) + source
    square_panel = lax.all_gather(square, "col", axis=1, tiled=True)
    operator_fourth = folder(square_panel, lax.all_gather(square, "row", axis=0, tiled=True))
    return (state_next, operator_fourth)


def solution(mesh):
    in_specs = (P("row", "col"), P("row", "col"), P("row", "col"))
    out_specs = (P("row", "col"), P("row", "col"))
    return jax.shard_map(
        on_device, mesh=mesh, in_specs=in_specs, out_specs=out_specs, check_vma=False
    )
```

profile of v0, /device:TPU:0, one launch (start us, length us, event | category | flops | bytes accessed | tf_op | source)
XLA Modules:
  0.0 784.8 jit_solution(5429908569219231628)
XLA Ops:
  7.2 0.7 all-gather.9.cloned.1.call-update
  7.9 0.7 all-gather.7.cloned.1.call-update
  8.7 0.7 all-gather.13.cloned.1.call-update
  9.4 0.0 all-gather.11.cloned.1.call-start
  9.4 90.6 %all-gather.9.cloned.1.call-done = f32[4096,512]{1,0:T(8,128)} async-done(((f32[1024,512]{1,0:T(8,128)}), f32[4096,512]{1,0:T(8,128)}) %all-gather.9.cloned.1.call-update) | async-done | bytes 8388624 | tf_op jit(solution)/shard_map/all_gather | solution.py:31
  100.1 152.7 %all-gather.7.cloned.1.call-done = f32[1024,4096]{1,0:T(8,128)} async-done(((f32[1024,512]{1,0:T(8,128)}), f32[1024,4096]{1,0:T(8,128)}) %all-gather.7.cloned.1.call-update) | async-done | bytes 16777232 | tf_op jit(solution)/shard_map/all_gather | solution.py:30
  252.8 31.0 %fusion = f32[1024,512]{1,0:T(8,128)} fusion(f32[1024,4096]{1,0:T(8,128)} %all-gather.7.cloned.1.call-done, f32[4096,512]{1,0:T(8,128)} %all-gather.9.cloned.1.call-done), kind=kOutput, calls=%fused_computation.1 | convolution fusion | flops 25769803776 | bytes 27262976 | tf_op jit(solution)/shard_map/dot_general | solution.py:8
  283.7 1.9 reshape.16
  285.7 1.8 copy.7
  287.5 51.3 %all_to_all.15 = f32[8,128,512]{2,1,0:T(8,128)S(1)} all-to-all(f32[8,128,512]{2,1,0:T(8,128)} %bitcast.18), channel_id=1, replica_groups=mesh['row'=4,'col'=8] {'row'}, dimensions={0} | all-to-all | bytes 4194304 | tf_op jit(solution)/shard_map/all_to_all | solution.py:34
  338.8 51.5 %all_to_all.16 = f32[8,128,512]{2,1,0:T(8,128)S(1)} all-to-all(f32[8,128,512]{2,1,0:T(8,128)S(1)} %all_to_all.15), channel_id=1, replica_groups=mesh['row'=4,'col'=8] {'col'}, dimensions={0} | all-to-all | bytes 4194304 | tf_op jit(solution)/shard_map/all_to_all | solution.py:33
  390.3 27.7 %all_to_all.17 = f32[8,128,512]{2,1,0:T(8,128)S(1)} all-to-all(f32[8,128,512]{2,1,0:T(8,128)S(1)} %all_to_all.16), channel_id=1, replica_groups=mesh['row'=4,'col'=8] {'row'}, dimensions={0} | all-to-all | bytes 4194304 | tf_op jit(solution)/shard_map/all_to_all | solution.py:43
  418.0 1.6 copy.8
  419.6 0.2 all-gather.17.cloned.1.call-start
  419.9 31.1 %fusion.1 = f32[1024,512]{1,0:T(8,128)} fusion(f32[1024,4096]{1,0:T(8,128)} %all-gather.7.cloned.1.call-done, f32[4096,512]{1,0:T(8,128)} %all-gather.13.cloned.1.call-done), kind=kOutput, calls=%fused_computation.2 | convolution fusion | flops 25769803776 | bytes 27262976 | tf_op jit(solution)/shard_map/dot_general | solution.py:8
  451.0 0.0 all-gather.15.cloned.1.call-start
  451.0 0.5 all-gather.15.cloned.1.call-update
  451.6 1.8 copy.9
  453.4 51.8 %all-gather.11.cloned.1.call-done = f32[4096,512]{1,0:T(8,128)} async-done(((f32[1024,512]{1,0:T(8,128)}), f32[4096,512]{1,0:T(8,128)}) %all-gather.11.cloned.1.call-update) | async-done | bytes 8388624 | tf_op jit(solution)/shard_map/all_gather | solution.py:45
  505.2 56.7 %bitcast_add_fusion = f32[1024,512]{0,1:T(8,128)S(1)} fusion(f32[1024,512]{0,1:T(8,128)} %copy.9, f32[4096,512]{1,0:T(8,128)} %all-gather.11.cloned.1.call-done, f32[1024,4096]{1,0:T(8,128)} %all-gather.7.cloned.1.call-done), kind=kOutput, calls=%fused_computation | convolution fusion | flops 25770328064 | bytes 29360128 | tf_op jit(solution)/shard_map/dot_general | solution.py:8
  562.0 1.8 copy.10
  563.8 30.6 %all-gather.17.cloned.1.call-done = f32[4096,512]{1,0:T(8,128)} async-done(((f32[1024,512]{1,0:T(8,128)}), f32[4096,512]{1,0:T(8,128)}) %all-gather.17.cloned.1.call-update) | async-done | bytes 8388624 | tf_op jit(solution)/shard_map/all_gather | solution.py:47
  594.4 152.6 %all-gather.15.cloned.1.call-done = f32[1024,4096]{1,0:T(8,128)} async-done(((f32[1024,512]{1,0:T(8,128)}), f32[1024,4096]{1,0:T(8,128)}) %all-gather.15.cloned.1.call-update) | async-done | bytes 16777232 | tf_op jit(solution)/shard_map/all_gather | solution.py:46
  747.0 31.0 %fusion.2 = f32[1024,512]{1,0:T(8,128)} fusion(f32[1024,4096]{1,0:T(8,128)} %all-gather.15.cloned.1.call-done, f32[4096,512]{1,0:T(8,128)} %all-gather.17.cloned.1.call-done), kind=kOutput, calls=%fused_computation.3 | convolution fusion | flops 25769803776 | bytes 27262976 | tf_op jit(solution)/shard_map/dot_general | solution.py:8
  (8 shorter events, 0.2 us)
Async XLA Ops:
  7.2 92.9 %all-gather.9.cloned.1.call-start = ((), (), s32[]{:S(2)}) async-start(), calls=%async_computation.4 | async-start | bytes 10485760 | tf_op jit(solution)/shard_map/all_gather | solution.py:31
  7.9 244.9 %all-gather.7.cloned.1.call-start = ((), (), s32[]{:S(2)}) async-start(), calls=%async_computation.3 | async-start | bytes 18874368 | tf_op jit(solution)/shard_map/all_gather | solution.py:30
  8.6 411.2 %all-gather.13.cloned.1.call-start = ((), (), s32[]{:S(2)}) async-start(), calls=%async_computation.6 | async-start | bytes 10485760 | tf_op jit(solution)/shard_map/all_gather | solution.py:32
  9.4 495.9 %all-gather.11.cloned.1.call-start = ((), (), s32[]{:S(2)}) async-start(), calls=%async_computation.5 | async-start | bytes 10485760 | tf_op jit(solution)/shard_map/all_gather | solution.py:45
  419.6 32.0 %copy-start = (f32[1024,512]{1,0:T(8,128)S(1)}, f32[1024,512]{1,0:T(8,128)}, u32[]{:S(2)}) copy-start(f32[1024,512]{1,0:T(8,128)} %param.5) | copy-start | bytes 6291460
  419.6 174.8 %all-gather.17.cloned.1.call-start = ((), (), s32[]{:S(2)}) async-start(), calls=%async_computation.8 | async-start | bytes 10485760 | tf_op jit(solution)/shard_map/all_gather | solution.py:47
  451.0 296.0 %all-gather.15.cloned.1.call-start = ((), (), s32[]{:S(2)}) async-start(), calls=%async_computation.7 | async-start | bytes 18874368 | tf_op jit(solution)/shard_map/all_gather | solution.py:46
Sparse Core Ops, SparseCore 0:
  9.8 90.1 all-gather.8
  101.7 151.0 all-gather.6
  254.6 107.1 all-gather.12
  419.7 85.4 all-gather.10
  506.9 87.4 all-gather.16
  595.9 151.0 all-gather.14
where the time goes:
time: 785 us
  waiting for transfers between devices  481 us (61%)
  matrix products  150 us (19%)
  blocking collectives  131 us (17%)
  between operations  14.2 us (2%)
  local copies, waits for them, and re-layouts  8.94 us (1%)
    all_gather x1, waiting for transfers between devices, on_device(): row_panel = lax.all_gather(operator, 'col', axis=1, tiled=True)  153 us
    all_gather x1, waiting for transfers between devices, on_device(): square_panel = lax.all_gather(square, 'col', axis=1, tiled=True)  153 us
    dot_general x4, matrix products, matmul(): jnp.dot(left, right, preferred_element_type=jnp.float32, precision=lax.Pr...  150 us
    all_gather x1, waiting for transfers between devices, on_device(): lax.all_gather(state, 'row', axis=0, tiled=True)  90.6 us
    all_gather x1, waiting for transfers between devices, on_device(): lax.all_gather(turned, 'row', axis=0, tiled=True)  51.8 us
    all_to_all x1, blocking collectives, on_device(): lax.all_to_all(lax.all_to_all(split_pieces(product, groups), 'row', split...  51.5 us
    all_to_all x1, blocking collectives, on_device(): lax.all_to_all(split_pieces(product, groups), 'row', split_axis=0, concat...  51.3 us
    all_gather x1, waiting for transfers between devices, on_device(): lax.all_gather(square, 'row', axis=0, tiled=True)  30.6 us
  transfers between devices with their start and end apart: 6, of which 5 were waited for; matrix products, arithmetic and copies ran while one was open for 16% of the time, Pallas kernels for 0%

commit v1 on v0

--- a/solution.py
+++ b/solution.py
@@ -2,6 +2,8 @@
 import jax.numpy as jnp
 from jax import lax
 from jax.sharding import PartitionSpec as P
+
+press_heads = lambda inputs, dev_axis: jnp.concatenate(lax.all_gather(inputs, dev_axis), 1)
 
 
 def matmul(left, right):
@@ -27,7 +29,7 @@
 
 def on_device(operator, state, source):
     groups = lax.axis_size("row")
-    row_panel = lax.all_gather(operator, "col", axis=1, tiled=True)
+    row_panel = press_heads(operator, "col")
     product = matmul(row_panel, lax.all_gather(state, "row", axis=0, tiled=True))
     square = matmul(row_panel, lax.all_gather(operator, "row", axis=0, tiled=True))
     moved = lax.all_to_all(

time: 785 us -> 834 us (1.062); the launches traced: 785 us -> 825 us
  local copies, waits for them, and re-layouts: 8.94 us -> 65.1 us
  waiting for transfers between devices: 481 us -> 460 us
    dot_general x0 -> x2, local copies, waits for them, and re-layouts: none -> 27.2 us  [matmul(): jnp.dot(left, right, preferred_element_type=jnp.float32, precision=lax.Pr...]
    all_gather x0 -> x1, local copies, waits for them, and re-layouts: none -> 18.3 us  [lax.all_gather(inputs, dev_axis)]
    all_to_all x1, blocking collectives: 51.5 us -> 66.8 us  [on_device(): lax.all_to_all(lax.all_to_all(split_pieces(product, groups), 'row', split...]
    unnamed x4 -> x5, local copies, waits for them, and re-layouts: 3.63 us -> 16.2 us
    all_gather x1, waiting for transfers between devices: 51.8 us -> 39.4 us  [on_device(): lax.all_gather(turned, 'row', axis=0, tiled=True)]
    all_to_all x1, blocking collectives: 51.3 us -> 40.8 us  [on_device(): lax.all_to_all(split_pieces(product, groups), 'row', split_axis=0, concat...]
    all_gather x1, waiting for transfers between devices: 153 us -> 144 us  [lax.all_gather(inputs, dev_axis)]
  transfers between devices with their start and end apart: 6 -> 6, of which waited for: 5 -> 5; matrix products, arithmetic and copies ran while one was open for 16% -> 22% of each run, Pallas kernels for 0% -> 0%
where the time goes in v1:
time: 834 us; the launch traced here: 825 us
  waiting for transfers between devices  460 us (55%)
  matrix products  150 us (18%)
  blocking collectives  135 us (16%)
  local copies, waits for them, and re-layouts  65.1 us (8%)
  between operations  14.5 us (2%)
    all_gather x1, waiting for transfers between devices, on_device(): square_panel = lax.all_gather(square, 'col', axis=1, tiled=True)  153 us
    dot_general x4, matrix products, matmul(): jnp.dot(left, right, preferred_element_type=jnp.float32, precision=lax.Pr...  150 us
    all_gather x1, waiting for transfers between devices, lax.all_gather(inputs, dev_axis)  144 us
    all_gather x1, waiting for transfers between devices, on_device(): lax.all_gather(state, 'row', axis=0, tiled=True)  90.6 us
    all_to_all x1, blocking collectives, on_device(): lax.all_to_all(lax.all_to_all(split_pieces(product, groups), 'row', split...  66.8 us
    all_to_all x1, blocking collectives, on_device(): lax.all_to_all(split_pieces(product, groups), 'row', split_axis=0, concat...  40.8 us
    all_gather x1, waiting for transfers between devices, on_device(): lax.all_gather(turned, 'row', axis=0, tiled=True)  39.4 us
    all_gather x1, waiting for transfers between devices, on_device(): lax.all_gather(square, 'row', axis=0, tiled=True)  30.7 us
  transfers between devices with their start and end apart: 6, of which 5 were waited for; matrix products, arithmetic and copies ran while one was open for 22% of the time, Pallas kernels for 0%

profile of v1, /device:TPU:0, one launch (start us, length us, event | category | flops | bytes accessed | tf_op | source)
XLA Modules:
  0.0 824.7 jit_solution(14138794523996968435)
XLA Ops:
  7.2 0.7 all-gather.8.cloned.1.call-update
  7.9 0.7 all-gather.18.cloned.1.call-update
  8.7 0.7 all-gather.12.cloned.1.call-update
  9.4 90.6 %all-gather.8.cloned.1.call-done = f32[4096,512]{1,0:T(8,128)} async-done(((f32[1024,512]{1,0:T(8,128)}), f32[4096,512]{1,0:T(8,128)}) %all-gather.8.cloned.1.call-update) | async-done | bytes 8388624 | tf_op jit(solution)/shard_map/all_gather | solution.py:33
  100.1 8.9 %copy.10 = f32[512,4096]{1,0:T(8,128)} copy(f32[512,4096]{0,1:T(8,128)} %bitcast.38) | data formatting | bytes 16777216 | tf_op jit(solution)/shard_map/dot_general | solution.py:10
  109.0 143.8 %all-gather.18.cloned.1.call-done = f32[8192,512]{1,0:T(8,128)} async-done(((f32[1024,512]{1,0:T(8,128)}), f32[8192,512]{1,0:T(8,128)}) %all-gather.18.cloned.1.call-update) | async-done | bytes 16777232 | tf_op jit(solution)/shard_map/all_gather | solution.py:6
  252.8 18.3 %copy.19 = f32[8,1024,512]{2,0,1:T(8,128)} copy(f32[8,1024,512]{2,1,0:T(8,128)} %bitcast.33) | data formatting | bytes 33554432 | tf_op jit(solution)/shard_map/all_gather | solution.py:6
  271.0 18.2 %reshape.29 = f32[2,512,4096,1]{2,1,0,3:T(8,128)} reshape(f32[1024,8,512]{2,1,0:T(8,128)} %bitcast.35) | data formatting | bytes 33554432 | tf_op jit(solution)/shard_map/dot_general | solution.py:10
  289.3 31.0 %fusion.2 = f32[4,2,128,512]{2,3,0,1:T(8,128)} fusion(f32[4,128,4096,1]{2,1,0,3:T(8,128)} %bitcast.39, f32[2,512,4096,1]{2,1,0,3:T(8,128)} %reshape.29), kind=kOutput, calls=%fused_computation.3 | convolution fusion | flops 25769803776 | bytes 27262976 | tf_op jit(solution)/shard_map/dot_general | solution.py:10
  320.3 1.9 copy.11
  322.2 40.8 %all_to_all.15 = f32[8,128,512]{2,1,0:T(8,128)S(1)} all-to-all(f32[8,128,512]{2,1,0:T(8,128)S(1)} %bitcast.41), channel_id=1, replica_groups=mesh['row'=4,'col'=8] {'row'}, dimensions={0} | all-to-all | bytes 4194304 | tf_op jit(solution)/shard_map/all_to_all | solution.py:36
  363.0 66.8 %all_to_all.16 = f32[8,128,512]{2,1,0:T(8,128)S(1)} all-to-all(f32[8,128,512]{2,1,0:T(8,128)S(1)} %all_to_all.15), channel_id=1, replica_groups=mesh['row'=4,'col'=8] {'col'}, dimensions={0} | all-to-all | bytes 4194304 | tf_op jit(solution)/shard_map/all_to_all | solution.py:35
  429.8 27.7 %all_to_all.17 = f32[8,128,512]{2,1,0:T(8,128)S(1)} all-to-all(f32[8,128,512]{2,1,0:T(8,128)S(1)} %all_to_all.16), channel_id=1, replica_groups=mesh['row'=4,'col'=8] {'row'}, dimensions={0} | all-to-all | bytes 4194304 | tf_op jit(solution)/shard_map/all_to_all | solution.py:45
  457.5 1.6 copy.12
  459.1 12.5 %copy.16 = f32[128,8,8,512]{3,1,2,0:T(8,128)} copy(f32[128,8,8,512]{3,1,0,2:T(8,128)} %bitcast.34) | data formatting | bytes 33554432
  471.7 31.2 %fusion.5 = f32[1024,512]{1,0:T(8,128)} fusion(f32[1024,4096]{1,0:T(8,128)} %bitcast.36, f32[4096,512]{1,0:T(8,128)} %all-gather.12.cloned.1.call-done), kind=kOutput, calls=%fused_computation.5 | convolution fusion | flops 25769803776 | bytes 27262976 | tf_op jit(solution)/shard_map/dot_general | solution.py:10
  502.9 0.5 all-gather.14.cloned.1.call-update
  503.5 1.8 copy.13
  505.3 39.4 %all-gather.10.cloned.1.call-done = f32[4096,512]{1,0:T(8,128)} async-done(((f32[1024,512]{1,0:T(8,128)}), f32[4096,512]{1,0:T(8,128)}) %all-gather.10.cloned.1.call-update) | async-done | bytes 8388624 | tf_op jit(solution)/shard_map/all_gather | solution.py:47
  544.7 56.7 %bitcast_add_fusion = f32[1024,512]{0,1:T(8,128)S(1)} fusion(f32[1024,512]{0,1:T(8,128)} %copy.13, f32[4096,512]{1,0:T(8,128)} %all-gather.10.cloned.1.call-done, f32[1024,4096]{1,0:T(8,128)} %bitcast.37), kind=kOutput, calls=%fused_computation.2 | convolution fusion | flops 25770328064 | bytes 29360128 | tf_op jit(solution)/shard_map/dot_general | solution.py:10
  601.4 1.8 copy.14
  603.2 30.7 %all-gather.16.cloned.1.call-done = f32[4096,512]{1,0:T(8,128)} async-done(((f32[1024,512]{1,0:T(8,128)}), f32[4096,512]{1,0:T(8,128)}) %all-gather.16.cloned.1.call-update) | async-done | bytes 8388624 | tf_op jit(solution)/shard_map/all_gather | solution.py:49
  633.9 152.6 %all-gather.14.cloned.1.call-done = f32[1024,4096]{1,0:T(8,128)} async-done(((f32[1024,512]{1,0:T(8,128)}), f32[1024,4096]{1,0:T(8,128)}) %all-gather.14.cloned.1.call-update) | async-done | bytes 16777232 | tf_op jit(solution)/shard_map/all_gather | solution.py:48
  786.5 31.0 %fusion.6 = f32[1024,512]{1,0:T(8,128)} fusion(f32[1024,4096]{1,0:T(8,128)} %all-gather.14.cloned.1.call-done, f32[4096,512]{1,0:T(8,128)} %all-gather.16.cloned.1.call-done), kind=kOutput, calls=%fused_computation.6 | convolution fusion | flops 25769803776 | bytes 27262976 | tf_op jit(solution)/shard_map/dot_general | solution.py:10
  (11 shorter events, 0.3 us)
Async XLA Ops:
  7.2 92.9 %all-gather.8.cloned.1.call-start = ((), (), s32[]{:S(2)}) async-start(), calls=%async_computation.3 | async-start | bytes 10485760 | tf_op jit(solution)/shard_map/all_gather | solution.py:33
  7.9 244.9 %all-gather.18.cloned.1.call-start = ((), (), s32[]{:S(2)}) async-start(), calls=%async_computation.8 | async-start | bytes 18874368 | tf_op jit(solution)/shard_map/all_gather | solution.py:6
  8.6 463.0 %all-gather.12.cloned.1.call-start = ((), (), s32[]{:S(2)}) async-start(), calls=%async_computation.5 | async-start | bytes 10485760 | tf_op jit(solution)/shard_map/all_gather | solution.py:34
  9.4 535.3 %all-gather.10.cloned.1.call-start = ((), (), s32[]{:S(2)}) async-start(), calls=%async_computation.4 | async-start | bytes 10485760 | tf_op jit(solution)/shard_map/all_gather | solution.py:47
  459.1 174.8 %all-gather.16.cloned.1.call-start = ((), (), s32[]{:S(2)}) async-start(), calls=%async_computation.7 | async-start | bytes 10485760 | tf_op jit(solution)/shard_map/all_gather | solution.py:49
  471.7 31.8 %copy-start = (f32[1024,512]{1,0:T(8,128)S(1)}, f32[1024,512]{1,0:T(8,128)}, u32[]{:S(2)}) copy-start(f32[1024,512]{1,0:T(8,128)} %param.5) | copy-start | bytes 6291460
  502.9 283.6 %all-gather.14.cloned.1.call-start = ((), (), s32[]{:S(2)}) async-start(), calls=%async_computation.6 | async-start | bytes 18874368 | tf_op jit(solution)/shard_map/all_gather | solution.py:48
Sparse Core Ops, SparseCore 0:
  9.8 90.1 all-gather.7
  101.6 151.0 all-gather.17
  254.6 107.3 all-gather.11
  459.2 85.4 all-gather.9
  546.4 87.4 all-gather.15
  635.4 151.0 all-gather.13
